TPU v7x, 32 devices: a whole 2x2x4 slice. The times are simulated.
32 devices in a mesh: gx: 4 (over y, core), gy: 4 (over z), gz: 2 (over x).
Axes of the slice: x: 2, y: 2, z: 4, core: 2. Of those that a mesh axis runs over, the one named last changes fastest.
Arguments:
- permittivity: float32 [32, 128, 256], P('gx', 'gy', 'gz'), may hold values from 1 to 9
- loss: float32 [32, 128, 256], P('gx', 'gy', 'gz'), may hold values from 0 to 0.2
- fwd_electric: float32 [3, 32, 128, 256], P(None, 'gx', 'gy', 'gz'), may hold values from -6 to 6
- fwd_magnetic: float32 [3, 32, 128, 256], P(None, 'gx', 'gy', 'gz'), may hold values from -6 to 6
- adj_electric: float32 [3, 32, 128, 256], P(None, 'gx', 'gy', 'gz'), may hold values from -200 to 200
- adj_magnetic: float32 [3, 32, 128, 256], P(None, 'gx', 'gy', 'gz'), may hold values from -200 to 200
- wavelet: float32 [64], replicated, may hold values from -6 to 6
- residuals: float32 [256, 64], P(('gx', 'gy', 'gz')), may hold values from -24 to 24
- source_cell: int32 [1], replicated, may hold values from 0 to 1048575
- receiver_cells: int32 [256], replicated, may hold values from 0 to 1048575
- start_step: int32 [1], replicated, may hold values from 0 to 60
Outputs:
- direction: float32 [32, 128, 256], P('gx', 'gy', 'gz')
- grad_rms: float32 [], replicated
Inputs may be any that keep to these rules, and one draw needn't show every extreme that they name: source_cell[0] is a flat index of a cell. receiver_cells[r] is the flat index of receiver r's cell; several receivers may share a cell. Samples start_step to start_step + 3 exist in every trace.
All inputs are finite; a program needn't handle non-finite values.
Results may differ from a plain program's by a relative error of at most 0.0003.
Values sent between devices are 32-bit elements; how exact they have to be, the bound alone decides.
A program may use at most 128 MiB of HBM per device.

v0:
```python
import jax
import jax.numpy as jnp
from jax import lax
from jax.sharding import PartitionSpec as P

STEPS = 4


def padded(cells, sides, width):
    for axis, dim in sides:
        count = lax.axis_size(axis)
        ends = count - 1
        head = lax.slice_in_dim(cells, 0, width, axis=dim)
        tail = lax.slice_in_dim(cells, cells.shape[dim] - width, cells.shape[dim], axis=dim)
        cells = jnp.concatenate(
            [
                lax.ppermute(tail, axis, [(i, (i + 1) % count) for i in range(ends)]),
                cells,
                lax.ppermute(head, axis, [((i + 1) % count, i) for i in range(ends)]),
            ],
            axis=dim,
        )
    return cells


def shifted_above(field, axis):
    rest = lax.slice_in_dim(field, 1, field.shape[axis], axis=axis)
    edge = jnp.zeros_like(lax.slice_in_dim(field, 0, 1, axis=axis))
    return jnp.concatenate([rest, edge], axis)


def shifted_below(field, axis):
    rest = lax.slice_in_dim(field, 0, field.shape[axis] - 1, axis=axis)
    edge = jnp.zeros_like(lax.slice_in_dim(field, 0, 1, axis=axis))
    return jnp.concatenate([edge, rest], axis)


def local_step(electric, magnetic, keep, curl, halved):
    electric_x, electric_y, electric_z = electric
    magnetic_x, magnetic_y, magnetic_z = magnetic
    magnetic_x = magnetic_x - halved * (
        shifted_above(electric_z, 1) - electric_z - (shifted_above(electric_y, 2) - electric_y)
    )
    magnetic_y = magnetic_y - halved * (
        shifted_above(electric_x, 2) - electric_x - (shifted_above(electric_z, 0) - electric_z)
    )
    magnetic_z = magnetic_z - halved * (
        shifted_above(electric_y, 0) - electric_y - (shifted_above(electric_x, 1) - electric_x)
    )
    electric_x = keep * electric_x + curl * (
        magnetic_z - shifted_below(magnetic_z, 1) - (magnetic_y - shifted_below(magnetic_y, 2))
    )
    electric_y = keep * electric_y + curl * (
        magnetic_x - shifted_below(magnetic_x, 2) - (magnetic_z - shifted_below(magnetic_z, 0))
    )
    electric_z = keep * electric_z + curl * (
        magnetic_y - shifted_below(magnetic_y, 0) - (magnetic_x - shifted_below(magnetic_x, 1))
    )
    return ((electric_x, electric_y, electric_z), (magnetic_x, magnetic_y, magnetic_z))


def interior(field, shape):
    return field[STEPS : STEPS + shape[0], STEPS : STEPS + shape[1], STEPS : STEPS + shape[2]]


def locate(flat, shape, totals, offsets):
    first = flat // (totals[1] * totals[2]) - offsets[0]
    second = flat // totals[2] % totals[1] - offsets[1]
    third = flat % totals[2] - offsets[2]
    inside = (
        (first >= 0)
        & (first < shape[0])
        & (second >= 0)
        & (second < shape[1])
        & (third >= 0)
        & (third < shape[2])
    )
    first = jnp.clip(first, 0, shape[0] - 1)
    second = jnp.clip(second, 0, shape[1] - 1)
    third = jnp.clip(third, 0, shape[2] - 1)
    return (first, second, third, inside)


def inject(electric, spot, values):
    first, second, third, inside = spot
    added = electric[2].at[first, second, third].add(jnp.where(inside, values, 0.0))
    return (electric[0], electric[1], added)


def correlate(snapshots, adjoints, shape):
    gradient = jnp.zeros(shape, jnp.float32)
    for index in range(STEPS):
        later = STEPS - index
        adjoint = adjoints[index]
        change = [snapshots[later][c] - snapshots[later - 1][c] for c in range(3)]
        gradient = gradient + (
            change[0] * adjoint[0] + change[1] * adjoint[1] + change[2] * adjoint[2]
        )
    return gradient


def per_device(
    permittivity,
    loss,
    fwd_electric,
    fwd_magnetic,
    adj_electric,
    adj_magnetic,
    wavelet,
    residuals,
    source_cell,
    receiver_cells,
    start_step,
):
    shape = permittivity.shape
    totals = (
        shape[0] * lax.axis_size("gx"),
        shape[1] * lax.axis_size("gy"),
        shape[2] * lax.axis_size("gz"),
    )
    offsets = (
        lax.axis_index("gx") * shape[0],
        lax.axis_index("gy") * shape[1],
        lax.axis_index("gz") * shape[2],
    )
    keep = (1.0 - loss) / (1.0 + loss)
    curl = 0.5 / (permittivity * (1.0 + loss))
    start = start_step[0]
    window = lax.dynamic_slice_in_dim(residuals, start, STEPS, 1)
    samples = lax.all_gather(window, ("gx", "gy", "gz"), axis=0, tiled=True)
    forward = (
        (fwd_electric[0], fwd_electric[1], fwd_electric[2]),
        (fwd_magnetic[0], fwd_magnetic[1], fwd_magnetic[2]),
    )
    snapshots = [forward[0]]
    adjoints = []
    stacked = jnp.concatenate(
        [fwd_electric, fwd_magnetic, adj_electric, adj_magnetic, keep[None], curl[None]], 0
    )
    widened = padded(stacked, (("gx", 1), ("gy", 2), ("gz", 3)), STEPS)
    wide_shape = widened.shape[1:]
    wide_offsets = tuple((offset - STEPS for offset in offsets))
    masks = []
    for axis_number in range(3):
        position = jnp.arange(wide_shape[axis_number], dtype=jnp.int32) + wide_offsets[axis_number]
        masks.append((position >= 0) & (position < totals[axis_number]))
    in_grid = masks[0][:, None, None] & masks[1][None, :, None] & masks[2][None, None, :]
    halved = jnp.where(in_grid, 0.5, 0.0).astype(jnp.float32)
    wide_keep = widened[12]
    wide_curl = widened[13]
    source_spot = locate(source_cell[0], wide_shape, totals, wide_offsets)
    receiver_spot = locate(receiver_cells, wide_shape, totals, wide_offsets)
    electric = (widened[0], widened[1], widened[2])
    magnetic = (widened[3], widened[4], widened[5])
    for index in range(STEPS):
        electric, magnetic = local_step(electric, magnetic, wide_keep, wide_curl, halved)
        pulse = lax.dynamic_slice_in_dim(wavelet, start + index, 1)[0]
        electric = inject(electric, source_spot, pulse)
        snapshots.append(tuple((interior(component, shape) for component in electric)))
    electric = (widened[6], widened[7], widened[8])
    magnetic = (widened[9], widened[10], widened[11])
    for index in range(STEPS):
        electric, magnetic = local_step(electric, magnetic, wide_keep, wide_curl, halved)
        electric = inject(electric, receiver_spot, samples[:, STEPS - 1 - index])
        adjoints.append(tuple((interior(component, shape) for component in electric)))
    gradient = -correlate(snapshots, adjoints, shape) / permittivity
    total = lax.psum(jnp.sum(gradient * gradient), ("gx", "gy", "gz"))
    grad_rms = jnp.sqrt(total / (totals[0] * totals[1] * totals[2]) + 1e-06)
    return (gradient / grad_rms, grad_rms)


def solution(mesh):
    placed = (
        P("gx", "gy", "gz"),
        P("gx", "gy", "gz"),
        P(None, "gx", "gy", "gz"),
        P(None, "gx", "gy", "gz"),
        P(None, "gx", "gy", "gz"),
        P(None, "gx", "gy", "gz"),
        P(),
        P(("gx", "gy", "gz"), None),
        P(),
        P(),
        P(),
    )
    return jax.shard_map(
        per_device,
        mesh=mesh,
        in_specs=placed,
        out_specs=(P("gx", "gy", "gz"), P()),
        check_vma=False,
    )
```

profile of v0, /device:TPU:0, one launch (start us, length us, event | category | flops | bytes accessed | tf_op | source)
XLA Modules:
  0.0 362.0 jit_solution(15681251726599199978)
XLA Ops:
  0.7 1.0 constant_dynamic-update-slice_fusion.3
  1.7 1.0 constant_dynamic-update-slice_fusion.2
  2.7 1.0 constant_dynamic-update-slice_fusion.1
  3.8 1.0 constant_dynamic-update-slice_fusion
  4.8 0.9 bitcast_dynamic-update-slice_fusion.1
  5.7 1.0 bitcast_dynamic-update-slice_fusion
  6.7 1.4 fusion.62
  8.2 2.4 collective-permute-start
  10.6 1.3 collective-permute-start.1
  12.8 71.8 %all-gather = f32[32,8,4]{1,2,0:T(4,128)S(1)} all-gather(f32[1,8,4]{1,2,0:T(4,128)S(1)} %bitcast.289), channel_id=1, replica_groups=mesh['gx'=4,'gy'=4,'gz'=2] {'gx','gy','gz'}, dimensions={0}, use_global_device_ids=true | all-gather | bytes 4224 | tf_op jit(solution)/shard_map/all_gather | solution.py:130
  84.8 1.3 pad_maximum_fusion.4
  86.1 1.3 collective-permute-start.2
  87.4 1.3 collective-permute-start.3
  88.8 4.6 %collective-permute-done.2 = f32[14,16,4,128]{3,2,1,0:T(4,128)S(1)} collective-permute-done((f32[14,16,4,128]{3,2,1,0:T(4,128)S(1)}, f32[14,16,4,128]{3,2,1,0:T(4,128)S(1)}, u32[]{:S(2)}, u32[]{:S(2)}) %collective-permute-start.2) | collective-permute-done | bytes 458784 | tf_op jit(solution)/shard_map/ppermute | solution.py:17
  93.4 4.4 %collective-permute-done.3 = f32[14,16,4,128]{3,2,1,0:T(4,128)S(1)} collective-permute-done((f32[14,16,4,128]{3,2,1,0:T(4,128)S(1)}, f32[14,16,4,128]{3,2,1,0:T(4,128)S(1)}, u32[]{:S(2)}, u32[]{:S(2)}) %collective-permute-start.3) | collective-permute-done | bytes 458784 | tf_op jit(solution)/shard_map/ppermute | solution.py:19
  97.8 2.0 pad_maximum_fusion.1
  99.8 5.2 %fusion.61 = (f32[14,16,40,4]{3,2,1,0:T(8,128)}, f32[14,16,40,4]{3,2,1,0:T(8,128)}) fusion(f32[14,16,40,128]{3,2,1,0:T(8,128)S(1)} %pad_maximum_fusion.1), kind=kLoop, calls=%fused_computation.188 | loop fusion | bytes 573440 | tf_op jit(solution)/shard_map/slice | solution.py:14
  105.1 4.0 %copy.16 = f32[14,16,40,4]{2,1,3,0:T(8,128)} copy(f32[14,16,40,4]{3,2,1,0:T(8,128)} %get-tuple-element.95) | data formatting | bytes 286720 | tf_op jit(solution)/shard_map/slice | solution.py:14
  109.1 2.1 collective-permute-start.4
  111.2 4.0 %copy.17 = f32[14,16,40,4]{2,1,3,0:T(8,128)} copy(f32[14,16,40,4]{3,2,1,0:T(8,128)} %get-tuple-element.96) | data formatting | bytes 286720 | tf_op jit(solution)/shard_map/slice | solution.py:13
  115.1 1.3 collective-permute-start.5
  121.3 4.0 %copy.18 = f32[14,16,40,4]{3,2,1,0:T(8,128)} copy(f32[14,16,40,4]{2,1,3,0:T(8,128)} %collective-permute-done.4) | data formatting | bytes 286720 | tf_op jit(solution)/shard_map/ppermute | solution.py:17
  125.8 4.1 %copy.19 = f32[14,16,40,4]{3,2,1,0:T(8,128)} copy(f32[14,16,40,4]{2,1,3,0:T(8,128)} %collective-permute-done.5) | data formatting | bytes 286720 | tf_op jit(solution)/shard_map/ppermute | solution.py:19
  129.9 9.9 %pad_maximum_fusion = f32[14,16,40,136]{3,2,1,0:T(8,128)S(1)} fusion(f32[14,16,40,4]{3,2,1,0:T(8,128)} %copy.19, f32[14,16,4,128]{3,2,1,0:T(4,128)} %copy-done.62, f32[14,4,32,128]{3,2,1,0:T(8,128)} %collective-permute-done.1, f32[14,8,32,128]{3,2,1,0:T(8,128)S(1)} %bitcast_dynamic-update-slice_fusion, f32[14,4,32,128]{3,2,1,0:T(8,128)S(1)} %collective-permute-done, ...), kind=kLoop, calls=%fused_computation.4 | loop fusion | flops 7311360 | bytes 9748480 | tf_op jit(solution)/shard_map/concatenate | solution.py:15
  139.8 1.6 slice_bitcast_fusion.13
  142.6 1.7 fusion.1
  144.7 1.5 fusion
  146.3 1.0 multiply_add_fusion.10
  147.3 16.0 %scatter_fusion = f32[16,40,136]{2,1,0:T(8,128)S(1)} fusion(f32[16,40,136]{2,1,0:T(8,128)S(1)} %get-tuple-element.74, s32[256]{0:T(256)S(1)} %bitcast.253, f32[256]{0:T(256)S(1)} %get-tuple-element.129), kind=kCustom, calls=%fused_computation | custom fusion | flops 256 | bytes 6144 | tf_op jit(solution)/shard_map/scatter-add | solution.py:86
  165.1 3.7 %multiply_add_fusion.6 = (f32[16,40,136]{2,1,0:T(8,128)S(1)}, f32[16,40,136]{2,1,0:T(8,128)}, f32[16,40,136]{2,1,0:T(8,128)S(1)}) fusion(f32[16,40,136]{2,1,0:T(8,128)S(1)} %get-tuple-element.116, f32[16,40,135]{2,1,0:T(8,128)S(1)} %bitcast.279, f32[16,40,136]{2,1,0:T(8,128)S(1)} %get-tuple-element.117, f32[16,39,136]{2,1,0:T(8,128)S(1)} %bitcast.280, ...), kind=kLoop, calls=%fused_computation.74 | loop fusion | flops 1566720 | bytes 5852672 | tf_op jit(solution)/shard_map/add | solution.py:50
  168.8 16.2 %scatter_fusion.1 = f32[16,40,136]{2,1,0:T(8,128)S(1)} fusion(f32[16,40,136]{2,1,0:T(8,128)S(1)} %get-tuple-element.71, s32[256]{0:T(256)S(1)} %bitcast.254, f32[256]{0:T(256)S(1)} %get-tuple-element.128), kind=kCustom, calls=%fused_computation.1 | custom fusion | flops 256 | bytes 6144 | tf_op jit(solution)/shard_map/scatter-add | solution.py:86
  187.6 3.6 multiply_add_fusion.3
  191.2 16.0 %scatter_fusion.2 = f32[16,40,136]{2,1,0:T(8,128)S(1)} fusion(f32[16,40,136]{2,1,0:T(8,128)S(1)} %get-tuple-element.68, s32[256]{0:T(256)S(1)} %bitcast.255, f32[256]{0:T(256)S(1)} %get-tuple-element.127), kind=kCustom, calls=%fused_computation.2 | custom fusion | flops 256 | bytes 6144 | tf_op jit(solution)/shard_map/scatter-add | solution.py:86
  209.0 2.0 slice.840
  210.9 2.2 slice.842
  213.1 1.1 slice.851
  215.2 3.9 %multiply_add_fusion.19 = (f32[16,40,136]{2,1,0:T(8,128)}, f32[16,40,136]{2,1,0:T(8,128)}, f32[16,40,136]{2,1,0:T(8,128)S(1)}) fusion(f32[16,40,136]{2,1,0:T(8,128)S(1)} %copy-done.26, f32[16,40,135]{2,1,0:T(8,128)S(1)} %bitcast.269, f32[16,40,136]{2,1,0:T(8,128)S(1)} %copy-done.28, f32[16,39,136]{2,1,0:T(8,128)S(1)} %bitcast.270, ...), kind=kLoop, calls=%fused_computation.87 | loop fusion | flops 1566720 | bytes 5852672 | tf_op jit(solution)/shard_map/add | solution.py:50
  222.7 1.4 scatter-add.48
  224.1 1.3 slice.735
  225.4 1.2 slice.733
  226.5 1.1 slice.728
  227.7 1.3 slice.730
  230.1 3.9 %multiply_add_fusion.16 = (f32[16,40,136]{2,1,0:T(8,128)}, f32[16,40,136]{2,1,0:T(8,128)}, f32[16,40,136]{2,1,0:T(8,128)S(1)}) fusion(f32[16,40,136]{2,1,0:T(8,128)S(1)} %get-tuple-element.109, f32[16,40,135]{2,1,0:T(8,128)S(1)} %bitcast.278, f32[16,40,136]{2,1,0:T(8,128)S(1)} %get-tuple-element.107, f32[16,39,136]{2,1,0:T(8,128)S(1)} %bitcast.277, ...), kind=kLoop, calls=%fused_computation.84 | loop fusion | flops 1566720 | bytes 5852672 | tf_op jit(solution)/shard_map/add | solution.py:50
  234.0 0.9 copy-done.9
  237.4 1.4 scatter-add.49
  238.8 1.3 slice.747
  240.1 1.2 slice.745
  241.3 1.1 slice.740
  242.4 1.3 slice.742
  244.9 3.9 %multiply_add_fusion.13 = (f32[16,40,136]{2,1,0:T(8,128)}, f32[16,40,136]{2,1,0:T(8,128)}, f32[16,40,136]{2,1,0:T(8,128)S(1)}) fusion(f32[16,40,136]{2,1,0:T(8,128)S(1)} %get-tuple-element.106, f32[16,40,135]{2,1,0:T(8,128)S(1)} %bitcast.276, f32[16,40,136]{2,1,0:T(8,128)S(1)} %get-tuple-element.104, f32[16,39,136]{2,1,0:T(8,128)S(1)} %bitcast.275, ...), kind=kLoop, calls=%fused_computation.81 | loop fusion | flops 1566720 | bytes 5852672 | tf_op jit(solution)/shard_map/add | solution.py:50
  252.1 1.4 scatter-add.50
  253.6 1.3 slice.777
  254.9 1.8 slice.757
  256.6 1.1 slice.752
  257.8 1.3 slice.754
  259.5 2.6 fusion.21
  262.3 1.4 fusion.9
  263.7 3.0 multiply_add_fusion.8
  270.0 1.4 scatter-add.51
  271.4 2.0 slice.853
  273.4 2.0 slice.780
  275.3 36.0 %scatter_fusion.3 = f32[16,40,136]{2,1,0:T(8,128)} fusion(f32[16,40,136]{2,1,0:T(8,128)} %get-tuple-element.90, s32[256]{0:T(256)S(1)} %bitcast.256, f32[256]{0:T(256)S(1)} %get-tuple-element.52), kind=kCustom, calls=%fused_computation.3 | custom fusion | flops 256 | bytes 6144 | tf_op jit(solution)/shard_map/scatter-add | solution.py:86
  311.4 6.1 %multiply_reduce_fusion = (f32[]{:T(128)}, f32[8,32,128]{2,1,0:T(8,128)S(1)}) fusion(f32[8,32,128]{2,1,0:T(8,128)S(1)} %copy-done.63, f32[16,40,136]{2,1,0:T(8,128)} %scatter_fusion.3, f32[3,8,32,128]{3,2,1,0:T(8,128)} %param.21, f32[15,40,136]{2,1,0:T(8,128)} %slice.853, f32[16,40,135]{2,1,0:T(8,128)} %bitcast.282, f32[16,40,136]{2,1,0:T(8,128)} %copy-done.48, ...), kind=kLoop, calls=%fused_computation.145 | loop fusion | flops 2064383 | bytes 7039492 | tf_op jit(solution)/shard_map/reduce_sum | solution.py:167
  317.4 42.1 %psum.7 = f32[]{:T(128)} all-reduce(f32[]{:T(128)} %get-tuple-element.50), channel_id=1, replica_groups=mesh['gx'=4,'gy'=4,'gz'=2] {'gx','gy','gz'}, use_global_device_ids=true, to_apply=%region_6.7 | all-reduce | flops 1 | bytes 8 | tf_op jit(solution)/shard_map/psum | solution.py:167
  (208 shorter events, 19.2 us)
Async XLA Ops:
  0.6 12.0 %copy-start = (f32[8,64]{1,0:T(8,128)S(1)}, f32[8,64]{1,0:T(8,128)}, u32[]{:S(2)}) copy-start(f32[8,64]{1,0:T(8,128)} %param.26) | copy-start | bytes 6148
  0.6 84.1 %copy-start.66 = (s32[256]{0:T(256)S(1)}, s32[256]{0:T(256)}, u32[]{:S(2)}) copy-start(s32[256]{0:T(256)} %param.28) | copy-start | bytes 3076
  8.2 76.6 %collective-permute-start = (f32[14,4,32,128]{3,2,1,0:T(8,128)}, f32[14,4,32,128]{3,2,1,0:T(8,128)S(1)}, u32[]{:S(2)}, u32[]{:S(2)}) collective-permute-start(f32[14,4,32,128]{3,2,1,0:T(8,128)} %get-tuple-element.99), channel_id=1, source_target_pairs={{0,8},{8,16},{16,24},{1,9},{9,17},{17,25},{2,10},{10,18},{18,26},{... | collective-permute-start | bytes 2752520 | tf_op jit(solution)/shard_map/ppermute | solution.py:17
  10.6 74.2 %collective-permute-start.1 = (f32[14,4,32,128]{3,2,1,0:T(8,128)}, f32[14,4,32,128]{3,2,1,0:T(8,128)}, u32[]{:S(2)}, u32[]{:S(2)}) collective-permute-start(f32[14,4,32,128]{3,2,1,0:T(8,128)} %get-tuple-element.100), channel_id=1, source_target_pairs={{8,0},{16,8},{24,16},{9,1},{17,9},{25,17},{10,2},{18,10},{26,18},{... | collective-permute-start | bytes 2752520 | tf_op jit(solution)/shard_map/ppermute | solution.py:19
  86.1 7.3 %collective-permute-start.2 = (f32[14,16,4,128]{3,2,1,0:T(4,128)S(1)}, f32[14,16,4,128]{3,2,1,0:T(4,128)S(1)}, u32[]{:S(2)}, u32[]{:S(2)}) collective-permute-start(f32[14,16,4,128]{3,2,1,0:T(4,128)S(1)} %get-tuple-element.97), channel_id=1, source_target_pairs={{0,2},{2,4},{4,6},{1,3},{3,5},{5,7},{8,10},{10,12},{12,14},{9,11},... | collective-permute-start | bytes 1376264 | tf_op jit(solution)/shard_map/ppermute | solution.py:17
  87.4 10.4 %collective-permute-start.3 = (f32[14,16,4,128]{3,2,1,0:T(4,128)S(1)}, f32[14,16,4,128]{3,2,1,0:T(4,128)S(1)}, u32[]{:S(2)}, u32[]{:S(2)}) collective-permute-start(f32[14,16,4,128]{3,2,1,0:T(4,128)S(1)} %get-tuple-element.98), channel_id=1, source_target_pairs={{2,0},{4,2},{6,4},{3,1},{5,3},{7,5},{10,8},{12,10},{14,12},{11,9},... | collective-permute-start | bytes 1376264 | tf_op jit(solution)/shard_map/ppermute | solution.py:19
  97.8 7.3 %copy-start.62 = (f32[14,16,4,128]{3,2,1,0:T(4,128)}, f32[14,16,4,128]{3,2,1,0:T(4,128)S(1)}, u32[]{:S(2)}) copy-start(f32[14,16,4,128]{3,2,1,0:T(4,128)S(1)} %collective-permute-done.3) | copy-start | bytes 1376260
  105.1 12.1 %copy-start.65 = (f32[64]{0:T(128)S(1)}, f32[64]{0:T(128)}, u32[]{:S(2)}) copy-start(f32[64]{0:T(128)} %param.25) | copy-start | bytes 772
  105.1 15.5 %copy-start.67 = (s32[3]{0:T(128)S(1)}, s32[3]{0:T(128)}, u32[]{:S(2)}) copy-start(s32[3]{0:T(128)} %constant.209.clone.1) | copy-start | bytes 40
  109.1 12.2 %collective-permute-start.4 = (f32[14,16,40,4]{2,1,3,0:T(8,128)}, f32[14,16,40,4]{2,1,3,0:T(8,128)}, u32[]{:S(2)}, u32[]{:S(2)}) collective-permute-start(f32[14,16,40,4]{2,1,3,0:T(8,128)} %copy.16), channel_id=1, source_target_pairs={{0,1},{2,3},{4,5},{6,7},{8,9},{10,11},{12,13},{14,15},{16,17},{18,... | collective-permute-start | bytes 430088 | tf_op jit(solution)/shard_map/ppermute | solution.py:17
  115.1 10.7 %collective-permute-start.5 = (f32[14,16,40,4]{2,1,3,0:T(8,128)}, f32[14,16,40,4]{2,1,3,0:T(8,128)}, u32[]{:S(2)}, u32[]{:S(2)}) collective-permute-start(f32[14,16,40,4]{2,1,3,0:T(8,128)} %copy.17), channel_id=1, source_target_pairs={{1,0},{3,2},{5,4},{7,6},{9,8},{11,10},{13,12},{15,14},{17,16},{19,... | collective-permute-start | bytes 430088 | tf_op jit(solution)/shard_map/ppermute | solution.py:19
  139.8 6.4 %copy-start.2 = (f32[14,16,40,136]{3,2,1,0:T(8,128)}, f32[14,16,40,136]{3,2,1,0:T(8,128)S(1)}, u32[]{:S(2)}) copy-start(f32[14,16,40,136]{3,2,1,0:T(8,128)S(1)} %pad_maximum_fusion) | copy-start | bytes 14622724
  147.2 17.8 %copy-start.11 = (f32[16,40,136]{2,1,0:T(8,128)}, f32[16,40,136]{2,1,0:T(8,128)S(1)}, u32[]{:S(2)}) copy-start(f32[16,40,136]{2,1,0:T(8,128)S(1)} %get-tuple-element.73) | copy-start | bytes 1044484
  164.9 3.9 %copy-start.24 = (f32[16,40,136]{2,1,0:T(8,128)}, f32[16,40,136]{2,1,0:T(8,128)S(1)}, u32[]{:S(2)}) copy-start(f32[16,40,136]{2,1,0:T(8,128)S(1)} %get-tuple-element.118) | copy-start | bytes 1044484
  164.9 3.9 %copy-start.44 = (f32[16,40,136]{2,1,0:T(8,128)}, f32[16,40,136]{2,1,0:T(8,128)S(1)}, u32[]{:S(2)}) copy-start(f32[16,40,136]{2,1,0:T(8,128)S(1)} %get-tuple-element.116) | copy-start | bytes 1044484
  164.9 3.9 %copy-start.46 = (f32[16,40,136]{2,1,0:T(8,128)}, f32[16,40,136]{2,1,0:T(8,128)S(1)}, u32[]{:S(2)}) copy-start(f32[16,40,136]{2,1,0:T(8,128)S(1)} %get-tuple-element.117) | copy-start | bytes 1044484
  168.8 16.6 %copy-start.12 = (f32[16,40,136]{2,1,0:T(8,128)S(1)}, f32[16,40,136]{2,1,0:T(8,128)}, u32[]{:S(2)}) copy-start(f32[16,40,136]{2,1,0:T(8,128)} %get-tuple-element.70) | copy-start | bytes 1044484
  187.1 4.1 %copy-start.18 = (f32[16,40,136]{2,1,0:T(8,128)}, f32[16,40,136]{2,1,0:T(8,128)S(1)}, u32[]{:S(2)}) copy-start(f32[16,40,136]{2,1,0:T(8,128)S(1)} %get-tuple-element.115) | copy-start | bytes 1044484
  187.1 4.1 %copy-start.32 = (f32[16,40,136]{2,1,0:T(8,128)}, f32[16,40,136]{2,1,0:T(8,128)S(1)}, u32[]{:S(2)}) copy-start(f32[16,40,136]{2,1,0:T(8,128)S(1)} %get-tuple-element.113) | copy-start | bytes 1044484
  187.1 4.1 %copy-start.34 = (f32[16,40,136]{2,1,0:T(8,128)}, f32[16,40,136]{2,1,0:T(8,128)S(1)}, u32[]{:S(2)}) copy-start(f32[16,40,136]{2,1,0:T(8,128)S(1)} %get-tuple-element.114) | copy-start | bytes 1044484
  207.2 6.0 %copy-start.54 = (f32[16,40,136]{2,1,0:T(8,128)S(1)}, f32[16,40,136]{2,1,0:T(8,128)}, u32[]{:S(2)}) copy-start(f32[16,40,136]{2,1,0:T(8,128)} %get-tuple-element.67) | copy-start | bytes 1044484
  207.2 7.9 %copy-start.26 = (f32[16,40,136]{2,1,0:T(8,128)S(1)}, f32[16,40,136]{2,1,0:T(8,128)}, u32[]{:S(2)}) copy-start(f32[16,40,136]{2,1,0:T(8,128)} %get-tuple-element.78) | copy-start | bytes 1044484
  207.2 8.0 %copy-start.28 = (f32[16,40,136]{2,1,0:T(8,128)S(1)}, f32[16,40,136]{2,1,0:T(8,128)}, u32[]{:S(2)}) copy-start(f32[16,40,136]{2,1,0:T(8,128)} %get-tuple-element.75) | copy-start | bytes 1044484
  208.1 7.1 %copy-start.16 = (f32[16,40,136]{2,1,0:T(8,128)S(1)}, f32[16,40,136]{2,1,0:T(8,128)}, u32[]{:S(2)}) copy-start(f32[16,40,136]{2,1,0:T(8,128)} %get-tuple-element.80) | copy-start | bytes 1044484
  224.0 5.0 %copy-start.14 = (f32[16,40,136]{2,1,0:T(8,128)S(1)}, f32[16,40,136]{2,1,0:T(8,128)}, u32[]{:S(2)}) copy-start(f32[16,40,136]{2,1,0:T(8,128)} %get-tuple-element.64) | copy-start | bytes 1044484
  224.0 5.3 %copy-start.3 = (f32[16,40,136]{2,1,0:T(8,128)S(1)}, f32[16,40,136]{2,1,0:T(8,128)}, u32[]{:S(2)}) copy-start(f32[16,40,136]{2,1,0:T(8,128)} %get-tuple-element.63) | copy-start | bytes 1044484
  224.1 5.3 %copy-start.8 = (f32[16,40,136]{2,1,0:T(8,128)S(1)}, f32[16,40,136]{2,1,0:T(8,128)}, u32[]{:S(2)}) copy-start(f32[16,40,136]{2,1,0:T(8,128)} %scatter-add.48) | copy-start | bytes 1044484
  224.1 5.3 %copy-start.17 = (f32[16,40,136]{2,1,0:T(8,128)S(1)}, f32[16,40,136]{2,1,0:T(8,128)}, u32[]{:S(2)}) copy-start(f32[16,40,136]{2,1,0:T(8,128)} %get-tuple-element.80) | copy-start | bytes 1044484
  224.1 5.3 %copy-start.27 = (f32[16,40,136]{2,1,0:T(8,128)S(1)}, f32[16,40,136]{2,1,0:T(8,128)}, u32[]{:S(2)}) copy-start(f32[16,40,136]{2,1,0:T(8,128)} %get-tuple-element.78) | copy-start | bytes 1044484
  224.1 5.3 %copy-start.29 = (f32[16,40,136]{2,1,0:T(8,128)S(1)}, f32[16,40,136]{2,1,0:T(8,128)}, u32[]{:S(2)}) copy-start(f32[16,40,136]{2,1,0:T(8,128)} %get-tuple-element.75) | copy-start | bytes 1044484
  230.0 4.0 %copy-start.22 = (f32[16,40,136]{2,1,0:T(8,128)}, f32[16,40,136]{2,1,0:T(8,128)S(1)}, u32[]{:S(2)}) copy-start(f32[16,40,136]{2,1,0:T(8,128)S(1)} %get-tuple-element.108) | copy-start | bytes 1044484
  230.0 4.0 %copy-start.40 = (f32[16,40,136]{2,1,0:T(8,128)}, f32[16,40,136]{2,1,0:T(8,128)S(1)}, u32[]{:S(2)}) copy-start(f32[16,40,136]{2,1,0:T(8,128)S(1)} %get-tuple-element.107) | copy-start | bytes 1044484
  230.0 4.0 %copy-start.42 = (f32[16,40,136]{2,1,0:T(8,128)}, f32[16,40,136]{2,1,0:T(8,128)S(1)}, u32[]{:S(2)}) copy-start(f32[16,40,136]{2,1,0:T(8,128)S(1)} %get-tuple-element.109) | copy-start | bytes 1044484
  238.8 5.0 %copy-start.15 = (f32[16,40,136]{2,1,0:T(8,128)S(1)}, f32[16,40,136]{2,1,0:T(8,128)}, u32[]{:S(2)}) copy-start(f32[16,40,136]{2,1,0:T(8,128)} %get-tuple-element.61) | copy-start | bytes 1044484
  238.8 5.3 %copy-start.4 = (f32[16,40,136]{2,1,0:T(8,128)S(1)}, f32[16,40,136]{2,1,0:T(8,128)}, u32[]{:S(2)}) copy-start(f32[16,40,136]{2,1,0:T(8,128)} %get-tuple-element.60) | copy-start | bytes 1044484
  238.8 5.3 %copy-start.10 = (f32[16,40,136]{2,1,0:T(8,128)S(1)}, f32[16,40,136]{2,1,0:T(8,128)}, u32[]{:S(2)}) copy-start(f32[16,40,136]{2,1,0:T(8,128)} %scatter-add.49) | copy-start | bytes 1044484
  238.8 5.3 %copy-start.23 = (f32[16,40,136]{2,1,0:T(8,128)S(1)}, f32[16,40,136]{2,1,0:T(8,128)}, u32[]{:S(2)}) copy-start(f32[16,40,136]{2,1,0:T(8,128)} %copy-done.22) | copy-start | bytes 1044484
  238.8 5.3 %copy-start.41 = (f32[16,40,136]{2,1,0:T(8,128)S(1)}, f32[16,40,136]{2,1,0:T(8,128)}, u32[]{:S(2)}) copy-start(f32[16,40,136]{2,1,0:T(8,128)} %copy-done.40) | copy-start | bytes 1044484
  238.8 5.3 %copy-start.43 = (f32[16,40,136]{2,1,0:T(8,128)S(1)}, f32[16,40,136]{2,1,0:T(8,128)}, u32[]{:S(2)}) copy-start(f32[16,40,136]{2,1,0:T(8,128)} %copy-done.42) | copy-start | bytes 1044484
  244.8 4.0 %copy-start.20 = (f32[16,40,136]{2,1,0:T(8,128)}, f32[16,40,136]{2,1,0:T(8,128)S(1)}, u32[]{:S(2)}) copy-start(f32[16,40,136]{2,1,0:T(8,128)S(1)} %get-tuple-element.105) | copy-start | bytes 1044484
  244.8 4.0 %copy-start.36 = (f32[16,40,136]{2,1,0:T(8,128)}, f32[16,40,136]{2,1,0:T(8,128)S(1)}, u32[]{:S(2)}) copy-start(f32[16,40,136]{2,1,0:T(8,128)S(1)} %get-tuple-element.104) | copy-start | bytes 1044484
  244.8 4.0 %copy-start.38 = (f32[16,40,136]{2,1,0:T(8,128)}, f32[16,40,136]{2,1,0:T(8,128)S(1)}, u32[]{:S(2)}) copy-start(f32[16,40,136]{2,1,0:T(8,128)S(1)} %get-tuple-element.106) | copy-start | bytes 1044484
  253.5 5.6 %copy-start.56 = (f32[16,40,136]{2,1,0:T(8,128)S(1)}, f32[16,40,136]{2,1,0:T(8,128)}, u32[]{:S(2)}) copy-start(f32[16,40,136]{2,1,0:T(8,128)} %get-tuple-element.58) | copy-start | bytes 1044484
  253.5 5.9 %copy-start.19 = (f32[16,40,136]{2,1,0:T(8,128)S(1)}, f32[16,40,136]{2,1,0:T(8,128)}, u32[]{:S(2)}) copy-start(f32[16,40,136]{2,1,0:T(8,128)} %copy-done.18) | copy-start | bytes 1044484
  253.5 5.9 %copy-start.33 = (f32[16,40,136]{2,1,0:T(8,128)S(1)}, f32[16,40,136]{2,1,0:T(8,128)}, u32[]{:S(2)}) copy-start(f32[16,40,136]{2,1,0:T(8,128)} %copy-done.32) | copy-start | bytes 1044484
  253.5 5.9 %copy-start.35 = (f32[16,40,136]{2,1,0:T(8,128)S(1)}, f32[16,40,136]{2,1,0:T(8,128)}, u32[]{:S(2)}) copy-start(f32[16,40,136]{2,1,0:T(8,128)} %copy-done.34) | copy-start | bytes 1044484
  253.5 5.9 %copy-start.50 = (f32[16,40,136]{2,1,0:T(8,128)S(1)}, f32[16,40,136]{2,1,0:T(8,128)}, u32[]{:S(2)}) copy-start(f32[16,40,136]{2,1,0:T(8,128)} %get-tuple-element.66) | copy-start | bytes 1044484
  253.5 5.9 %copy-start.55 = (f32[16,40,136]{2,1,0:T(8,128)S(1)}, f32[16,40,136]{2,1,0:T(8,128)}, u32[]{:S(2)}) copy-start(f32[16,40,136]{2,1,0:T(8,128)} %get-tuple-element.67) | copy-start | bytes 1044484
  253.5 5.9 %copy-start.57 = (f32[16,39,136]{2,1,0:T(8,128)S(1)}, f32[16,39,136]{2,1,0:T(8,128)}, u32[]{:S(2)}) copy-start(f32[16,39,136]{2,1,0:T(8,128)} %slice.850) | copy-start | bytes 1018372
  253.5 5.9 %copy-start.58 = (f32[16,39,136]{2,1,0:T(8,128)S(1)}, f32[16,39,136]{2,1,0:T(8,128)}, u32[]{:S(2)}) copy-start(f32[16,39,136]{2,1,0:T(8,128)} %slice.840) | copy-start | bytes 1018372
  253.5 5.9 %copy-start.59 = (f32[16,40,135]{2,1,0:T(8,128)S(1)}, f32[16,40,135]{2,1,0:T(8,128)}, u32[]{:S(2)}) copy-start(f32[16,40,135]{2,1,0:T(8,128)} %slice.842) | copy-start | bytes 1036804
  253.5 5.9 %copy-start.60 = (f32[16,40,135]{2,1,0:T(8,128)S(1)}, f32[16,40,135]{2,1,0:T(8,128)}, u32[]{:S(2)}) copy-start(f32[16,40,135]{2,1,0:T(8,128)} %slice.851) | copy-start | bytes 1036804
  253.6 5.9 %copy-start.61 = (f32[15,40,136]{2,1,0:T(8,128)S(1)}, f32[15,40,136]{2,1,0:T(8,128)}, u32[]{:S(2)}) copy-start(f32[15,40,136]{2,1,0:T(8,128)} %slice.843) | copy-start | bytes 979204
  259.5 2.7 copy-start.6
  259.5 2.7 copy-start.21
  259.5 2.7 copy-start.37
  259.5 2.7 copy-start.39
  259.5 2.7 copy-start.51
  262.2 1.5 copy-start.48
  262.2 1.5 copy-start.52
  263.6 3.1 copy-start.49
  263.6 3.1 copy-start.53
  266.7 44.7 %copy-start.63 = (f32[8,32,128]{2,1,0:T(8,128)S(1)}, f32[8,32,128]{2,1,0:T(8,128)}, u32[]{:S(2)}) copy-start(f32[8,32,128]{2,1,0:T(8,128)} %param.19) | copy-start | bytes 393220
  311.4 49.5 %copy-start.1 = (f32[8,64]{1,0:T(8,128)S(1)}, f32[8,64]{1,0:T(8,128)}, u32[]{:S(2)}) copy-start(f32[8,64]{1,0:T(8,128)} %param.26) | copy-start | bytes 6148
  (10 other events, 10.6 us)
where the time goes:
time: 364 us; the launch traced here: 362 us
  other arithmetic  140 us (38%)
  blocking collectives  114 us (31%)
  local copies, waits for them, and re-layouts  74 us (20%)
  between operations  15.3 us (4%)
  starting transfers between devices  9.69 us (3%)
  waiting for transfers between devices  9.55 us (3%)
    scatter-add x4, other arithmetic, inject(): electric[2].at[first, second, third].add(jnp.where(inside, values, 0.0))  84.1 us
    all_gather x1, blocking collectives, per_device(): samples = lax.all_gather(window, ('gx', 'gy', 'gz'), axis=0, tiled=True)  71.8 us
    psum x1, blocking collectives, per_device(): total = lax.psum(jnp.sum(gradient * gradient), ('gx', 'gy', 'gz'))  42.1 us
    slice x45, local copies, waits for them, and re-layouts, shifted_above(): rest = lax.slice_in_dim(field, 1, field.shape[axis], axis=axis)  26.8 us
    add x6, other arithmetic, local_step(): keep * electric_x  19.9 us
    concatenate x2, other arithmetic, padded(): jnp.concatenate([lax.ppermute(tail, axis, [(i, (i + 1) % count) for i in...  12 us
    slice x3, local copies, waits for them, and re-layouts, padded(): lax.slice_in_dim(cells, cells.shape[dim] - width, cells.shape[dim], axis=...  10.7 us
    unnamed x141, local copies, waits for them, and re-layouts  9.46 us
  transfers between devices with their start and end apart: 6, of which 3 were waited for; matrix products, arithmetic and copies ran while one was open for 3% of the time, Pallas kernels for 0%

commit v1 on v0

v1 whole, which is shorter than its diff:
```python
import functools

import jax
import jax.numpy as jnp
from jax import lax
from jax.experimental import pallas as pl
from jax.experimental.pallas import tpu as pltpu
from jax.sharding import PartitionSpec as P

STEPS = 4
MESH = pl.DeviceIdType.MESH
F32 = jnp.float32
HALF = 0.5


def kernel(
    sizes,
    wav_ref,
    src_ref,
    start_ref,
    cells_ref,
    perm_hbm,
    loss_hbm,
    fe_hbm,
    fm_hbm,
    ae_hbm,
    am_hbm,
    res_ref,
    out_ref,
    rms_ref,
    E,
    H,
    perm,
    loss,
    keep,
    curl,
    D,
    A,
    inj,
    R,
    grad,
    ysend,
    yrecv,
    zsend,
    zrecv,
    part,
    suma,
    sumb,
    load_sem,
    face_send,
    face_recv,
    ga_send,
    ga_recv,
    gb_send,
    gb_recv,
    ra_send,
    ra_recv,
    rb_send,
    rb_recv,
):
    gx, gy, gz = sizes
    nx, ny, nz = perm.shape
    pad = E.shape[3] - ny
    ix, iy, iz = lax.axis_index("gx"), lax.axis_index("gy"), lax.axis_index("gz")
    nplane = gy * gz
    plane = iy * gz + iz

    loads = [
        pltpu.make_async_copy(fe_hbm, E.at[0, :, 0:nx, 0:ny, :], load_sem.at[0]),
        pltpu.make_async_copy(ae_hbm, E.at[1, :, 0:nx, 0:ny, :], load_sem.at[1]),
        pltpu.make_async_copy(fm_hbm, H.at[0, :, 1 : nx + 1, pad : pad + ny, :], load_sem.at[2]),
        pltpu.make_async_copy(am_hbm, H.at[1, :, 1 : nx + 1, pad : pad + ny, :], load_sem.at[3]),
        pltpu.make_async_copy(loss_hbm, loss, load_sem.at[4]),
        pltpu.make_async_copy(perm_hbm, perm, load_sem.at[5]),
    ]
    for load in loads:
        load.start()

    plane_peers = []
    for d in range(1, nplane):
        q = lax.rem(plane + d, nplane)
        plane_peers.append((q, (ix, q // gz, lax.rem(q, gz))))
    line_peers = []
    for d in range(1, gx):
        q = lax.rem(ix + d, gx)
        line_peers.append((q, (q, iy, iz)))

    zero_plane = jnp.zeros((ny, nz), F32)
    for s in range(2):
        for c in range(3):
            E[s, c, nx, 0:ny, :] = zero_plane
            H[s, c, 0, pad : pad + ny, :] = zero_plane
    yrecv[...] = jnp.zeros(yrecv.shape, F32)
    zrecv[...] = jnp.zeros(zrecv.shape, F32)

    barrier = pltpu.get_barrier_semaphore()
    for _, dev in plane_peers + line_peers:
        pl.semaphore_signal(barrier, inc=1, device_id=dev, device_id_type=MESH)
    pl.semaphore_wait(barrier, len(plane_peers) + len(line_peers))

    def remote(src, dst, ssem, rsem, dev):
        return pltpu.make_async_remote_copy(
            src_ref=src, dst_ref=dst, send_sem=ssem, recv_sem=rsem,
            device_id=dev, device_id_type=MESH,
        )

    per = res_ref.shape[0]

    def rows_of(x, q, count):
        return pl.ds(pl.multiple_of((x * nplane + q) * per, 8), count)

    R[rows_of(ix, plane, per), :] = res_ref[...]
    gather_a = []
    for d, (q, dev) in enumerate(plane_peers):
        send = remote(res_ref, R.at[rows_of(ix, plane, per), :], ga_send.at[d], ga_recv.at[plane], dev)
        recv = remote(res_ref, R.at[rows_of(ix, q, per), :], ga_send.at[d], ga_recv.at[q], dev)
        send.start()
        gather_a.append((send, recv))

    def gather_mid():
        for send, recv in gather_a:
            recv.wait_recv()
        for d, (q, dev) in enumerate(line_peers):
            mine = R.at[rows_of(ix, 0, per * nplane), :]
            remote(mine, mine, gb_send.at[d], gb_recv.at[ix], dev).start()

    def gather_end():
        for d, (q, dev) in enumerate(line_peers):
            theirs = R.at[rows_of(q, 0, per * nplane), :]
            remote(theirs, theirs, gb_send.at[d], gb_recv.at[q], dev).wait()
        for send, recv in gather_a:
            send.wait_send()

    def faces(s, kind):
        low = kind == 0
        step = -1 if low else 1
        field = E if low else H
        rows = slice(0, ny) if low else slice(pad, pad + ny)
        from_x, to_x = (0, nx) if low else (nx, 0)
        idx = (ix, iy, iz)
        size = (gx, gy, gz)
        refs = (
            (field.at[s, 1:3, from_x, rows, :], field.at[s, 1:3, to_x, rows, :]),
            (ysend.at[kind, s], yrecv.at[kind, s]),
            (zsend.at[kind, s], zrecv.at[kind, s]),
        )
        out = []
        for a in range(3):
            if low:
                can_send, can_recv = idx[a] > 0, idx[a] < size[a] - 1
            else:
                can_send, can_recv = idx[a] < size[a] - 1, idx[a] > 0
            dev = [ix, iy, iz]
            dev[a] = jnp.clip(idx[a] + step, 0, size[a] - 1)
            copy = remote(refs[a][0], refs[a][1], face_send.at[kind, s, a], face_recv.at[kind, s, a], tuple(dev))
            out.append((copy, can_send, can_recv))
        return out

    def start(face, extra=None):
        copy, can_send, _ = face
        cond = can_send if extra is None else can_send & extra

        @pl.when(cond)
        def _():
            copy.start()

    def finish(face):
        copy, can_send, _ = face

        @pl.when(can_send)
        def _():
            copy.wait_send()

    def arrive(face):
        copy, _, can_recv = face

        @pl.when(can_recv)
        def _():
            copy.wait_recv()

    lane = lax.broadcasted_iota(jnp.int32, (ny, nz), 1)
    row = lax.broadcasted_iota(jnp.int32, (ny, nz), 0)

    def pack_column(acc, value, source, j):
        return jnp.where(lane == j, pltpu.roll(value, (j - source) % nz, 1), acc)

    def up_z(value, halo, j):
        return jnp.where(lane == nz - 1, pltpu.roll(halo, (nz - 1 - j) % nz, 1), pltpu.roll(value, nz - 1, 1))

    def down_z(value, halo, j):
        rolled = pltpu.roll(value, 1, 1)
        return jnp.where(lane == 0, pltpu.roll(halo, (nz - j) % nz, 1), rolled)

    def send_first(s):
        acc = jnp.zeros((ny, nz), F32)
        face = faces(s, 0)
        start(face[0])
        for p in range(nx):
            ysend[0, s, 0, p : p + 1, :] = E[s, 0, p, 0:1, :]
            ysend[0, s, 1, p : p + 1, :] = E[s, 2, p, 0:1, :]
            acc = pack_column(acc, E[s, 0, p, 0:ny, :], 0, p)
            acc = pack_column(acc, E[s, 1, p, 0:ny, :], 0, nx + p)
        zsend[0, s] = acc
        start(face[1])
        start(face[2])

    def update_h(s):
        came = faces(s, 0)
        going = faces(s, 1)
        for face in came:
            arrive(face)
        for p in range(nx):
            E[s, 0, p, ny : ny + 1, :] = yrecv[0, s, 0, p : p + 1, :]
            E[s, 2, p, ny : ny + 1, :] = yrecv[0, s, 1, p : p + 1, :]
        halo = zrecv[0, s]
        acc = jnp.zeros((ny, nz), F32)
        inner = slice(pad, pad + ny)
        for p in reversed(range(nx)):
            ex, ey, ez = E[s, 0, p, 0:ny, :], E[s, 1, p, 0:ny, :], E[s, 2, p, 0:ny, :]
            hx = H[s, 0, p + 1, inner, :] - HALF * (E[s, 2, p, 1 : ny + 1, :] - ez - (up_z(ey, halo, nx + p) - ey))
            hy = H[s, 1, p + 1, inner, :] - HALF * (up_z(ex, halo, p) - ex - (E[s, 2, p + 1, 0:ny, :] - ez))
            hz = H[s, 2, p + 1, inner, :] - HALF * (E[s, 1, p + 1, 0:ny, :] - ey - (E[s, 0, p, 1 : ny + 1, :] - ex))
            H[s, 0, p + 1, inner, :] = hx
            H[s, 1, p + 1, inner, :] = hy
            H[s, 2, p + 1, inner, :] = hz
            if p == nx - 1:
                start(going[0])
            ysend[1, s, 0, p : p + 1, :] = hx[ny - 1 : ny, :]
            ysend[1, s, 1, p : p + 1, :] = hz[ny - 1 : ny, :]
            acc = pack_column(acc, hx, nz - 1, p)
            acc = pack_column(acc, hy, nz - 1, nx + p)
        zsend[1, s] = acc
        start(going[1])
        start(going[2])

    src = src_ref[0]
    begin = start_ref[0]
    total_z, total_y = nz * gz, ny * gy
    src_i = lax.div(src, total_y * total_z) - ix * nx
    src_j = lax.rem(lax.div(src, total_z), total_y) - iy * ny
    src_k = lax.rem(src, total_z) - iz * nz
    src_mask = (row == src_j) & (lane == src_k)

    def update_e(s, k):
        came = faces(s, 1)
        going = faces(s, 0)
        for face in came:
            arrive(face)
        for face in going:
            finish(face)
        for p in range(nx):
            H[s, 0, p + 1, pad - 1 : pad, :] = yrecv[1, s, 0, p : p + 1, :]
            H[s, 2, p + 1, pad - 1 : pad, :] = yrecv[1, s, 1, p : p + 1, :]
        more = k < STEPS - 1
        halo = zrecv[1, s]
        acc = jnp.zeros((ny, nz), F32)
        inner = slice(pad, pad + ny)
        below = slice(pad - 1, pad + ny - 1)
        pulse = wav_ref[begin + k]
        for p in range(nx):
            hx, hy, hz = H[s, 0, p + 1, inner, :], H[s, 1, p + 1, inner, :], H[s, 2, p + 1, inner, :]
            kp, cl = keep[p], curl[p]
            ox, oy, oz = E[s, 0, p, 0:ny, :], E[s, 1, p, 0:ny, :], E[s, 2, p, 0:ny, :]
            ex = kp * ox + cl * (hz - H[s, 2, p + 1, below, :] - (hy - down_z(hy, halo, nx + p)))
            ey = kp * oy + cl * (hx - down_z(hx, halo, p) - (hz - H[s, 2, p, inner, :]))
            ez = kp * oz + cl * (hy - H[s, 1, p, inner, :] - (hx - H[s, 0, p + 1, below, :]))
            if s == 0:
                ez = ez + jnp.where(src_mask, jnp.where(src_i == p, pulse, 0.0), 0.0)
                D[k, 0, p] = ex - ox
                D[k, 1, p] = ey - oy
                D[k, 2, p] = ez - oz
            else:
                ez = ez + inj[k, p * ny : (p + 1) * ny, :]
                A[k, 0, p] = ex
                A[k, 1, p] = ey
                A[k, 2, p] = ez
            E[s, 0, p, 0:ny, :] = ex
            E[s, 1, p, 0:ny, :] = ey
            E[s, 2, p, 0:ny, :] = ez
            if p == 0:
                start(going[0], more)
            ysend[0, s, 0, p : p + 1, :] = ex[0:1, :]
            ysend[0, s, 1, p : p + 1, :] = ez[0:1, :]
            acc = pack_column(acc, ex, 0, p)
            acc = pack_column(acc, ey, 0, nx + p)
        zsend[0, s] = acc
        start(going[1], more)
        start(going[2], more)
        for face in came_out(s):
            finish(face)

    def came_out(s):
        return faces(s, 1)

    def injection():
        cells = cells_ref[...]
        count = cells.shape[1]
        i = lax.div(cells, total_y * total_z) - ix * nx
        j = lax.rem(lax.div(cells, total_z), total_y) - iy * ny
        k = lax.rem(cells, total_z) - iz * nz
        inside = (i >= 0) & (i < nx) & (j >= 0) & (j < ny)
        where = jnp.where(inside, i * ny + j, -1)
        rows = lax.broadcasted_iota(jnp.int32, (nx * ny, count), 0)
        spots = jnp.where(rows == where, 1.0, 0.0).astype(jnp.bfloat16)
        depth = lax.broadcasted_iota(jnp.int32, (nz, count), 0) == k
        trace = R.shape[1]
        pick_lane = lax.broadcasted_iota(jnp.int32, (8, trace), 1)
        pick_row = lax.broadcasted_iota(jnp.int32, (8, trace), 0)
        pick = jnp.where(pick_lane == begin + STEPS - 1 - pick_row, 1.0, 0.0)
        nt = (((1,), (1,)), ((), ()))
        samples = lax.dot_general(pick, R[...], nt, precision=lax.Precision.HIGHEST, preferred_element_type=F32)
        for m in range(STEPS):
            rest = jnp.where(depth, samples[m : m + 1, :], 0.0)
            total = jnp.zeros((nx * ny, nz), F32)
            for _ in range(3):
                head = rest.astype(jnp.bfloat16)
                rest = rest - head.astype(F32)
                total = total + lax.dot_general(spots, head, nt, preferred_element_type=F32)
            inj[m] = total

    loads[0].wait()
    send_first(0)
    loads[1].wait()
    send_first(1)
    loads[4].wait()
    loads[5].wait()
    for p in range(nx):
        lo = loss[p]
        keep[p] = (1.0 - lo) / (1.0 + lo)
        curl[p] = 0.5 / (perm[p] * (1.0 + lo))
    loads[2].wait()
    loads[3].wait()

    update_h(0)
    gather_mid()
    update_h(1)
    update_e(0, 0)
    gather_end()
    injection()
    update_e(1, 0)

    def body(k, carry):
        update_h(0)
        update_h(1)
        update_e(0, k)
        update_e(1, k)
        return carry

    lax.fori_loop(1, STEPS, body, 0)

    squares = jnp.zeros((ny, nz), F32)
    for p in range(nx):
        total = jnp.zeros((ny, nz), F32)
        for m in range(STEPS):
            n = STEPS - 1 - m
            total = total + (D[n, 0, p] * A[m, 0, p] + D[n, 1, p] * A[m, 1, p] + D[n, 2, p] * A[m, 2, p])
        g = -total / perm[p]
        grad[p] = g
        squares = squares + g * g
    tile = squares[0:8, :]
    for r in range(1, ny // 8):
        tile = tile + squares[8 * r : 8 * r + 8, :]
    part[0] = tile

    def reduce(src, slots, me, peers, send_sems, recv_sems, count):
        slots[pl.ds(me, 1)] = src[...][None]
        copies = []
        for d, (q, dev) in enumerate(peers):
            send = remote(src, slots.at[me], send_sems.at[d], recv_sems.at[me], dev)
            recv = remote(src, slots.at[q], send_sems.at[d], recv_sems.at[q], dev)
            send.start()
            copies.append((send, recv))
        for send, recv in copies:
            recv.wait_recv()
        out = slots[0]
        for q in range(1, count):
            out = out + slots[q]
        for send, recv in copies:
            send.wait_send()
        return out

    part[1] = reduce(part.at[0], suma, plane, plane_peers, ra_send, ra_recv, nplane)
    tile = reduce(part.at[1], sumb, ix, line_peers, rb_send, rb_recv, gx)
    total = jnp.sum(jnp.sum(tile, axis=0, keepdims=True), axis=1, keepdims=True)
    rms = jnp.sqrt(total / (nx * ny * nz * gx * gy * gz) + 1e-06)
    rms_ref[...] = rms
    inverse = 1.0 / rms
    for p in range(nx):
        out_ref[p] = grad[p] * inverse


def per_device(
    permittivity, loss, fwd_electric, fwd_magnetic, adj_electric, adj_magnetic,
    wavelet, residuals, source_cell, receiver_cells, start_step,
):
    sizes = tuple(lax.axis_size(a) for a in ("gx", "gy", "gz"))
    gx, gy, gz = sizes
    nx, ny, nz = permittivity.shape
    nplane = gy * gz
    count = receiver_cells.shape[0]
    trace = residuals.shape[1]
    smem = pl.BlockSpec(memory_space=pltpu.SMEM)
    vmem = pl.BlockSpec(memory_space=pltpu.VMEM)
    hbm = pl.BlockSpec(memory_space=pl.ANY)
    dma = pltpu.SemaphoreType.DMA
    block = (nx, ny, nz)
    padded = (2, 3, nx + 1, ny + 8, nz)
    direction, rms = pl.pallas_call(
        functools.partial(kernel, sizes),
        out_shape=(
            jax.ShapeDtypeStruct(block, F32),
            jax.ShapeDtypeStruct((1, 1), F32),
        ),
        in_specs=[smem, smem, smem, vmem, hbm, hbm, hbm, hbm, hbm, hbm, vmem],
        out_specs=(vmem, vmem),
        scratch_shapes=[
            pltpu.VMEM(padded, F32),
            pltpu.VMEM(padded, F32),
            pltpu.VMEM(block, F32),
            pltpu.VMEM(block, F32),
            pltpu.VMEM(block, F32),
            pltpu.VMEM(block, F32),
            pltpu.VMEM((STEPS, 3) + block, F32),
            pltpu.VMEM((STEPS, 3) + block, F32),
            pltpu.VMEM((STEPS, nx * ny, nz), F32),
            pltpu.VMEM((count, trace), F32),
            pltpu.VMEM(block, F32),
            pltpu.VMEM((2, 2, 2, nx, nz), F32),
            pltpu.VMEM((2, 2, 2, nx, nz), F32),
            pltpu.VMEM((2, 2, ny, nz), F32),
            pltpu.VMEM((2, 2, ny, nz), F32),
            pltpu.VMEM((2, 8, nz), F32),
            pltpu.VMEM((nplane, 8, nz), F32),
            pltpu.VMEM((gx, 8, nz), F32),
            dma((6,)),
            dma((2, 2, 3)),
            dma((2, 2, 3)),
            dma((nplane,)),
            dma((nplane,)),
            dma((gx,)),
            dma((gx,)),
            dma((nplane,)),
            dma((nplane,)),
            dma((gx,)),
            dma((gx,)),
        ],
        compiler_params=pltpu.CompilerParams(
            collective_id=0, has_side_effects=True, vmem_limit_bytes=60 * 1024 * 1024
        ),
    )(
        wavelet, source_cell, start_step, receiver_cells.reshape(1, count),
        permittivity, loss, fwd_electric, fwd_magnetic, adj_electric, adj_magnetic, residuals,
    )
    return direction, rms.reshape(())


def solution(mesh):
    block = P("gx", "gy", "gz")
    state = P(None, "gx", "gy", "gz")
    return jax.shard_map(
        per_device,
        mesh=mesh,
        in_specs=(
            block, block, state, state, state, state,
            P(), P(("gx", "gy", "gz"), None), P(), P(), P(),
        ),
        out_specs=(block, P()),
        check_vma=False,
    )
```

time: 364 us -> 48.6 us (0.13)
  other arithmetic: 140 us -> 0 us
  blocking collectives: 114 us -> 0 us
  local copies, waits for them, and re-layouts: 74 us -> 1.57 us
  Pallas kernels: 0 us -> 43.1 us
  between operations: 15.3 us -> 3.74 us
  starting transfers between devices: 9.69 us -> 0 us
  waiting for transfers between devices: 9.55 us -> 0 us
    scatter-add x4 -> x0, other arithmetic: 84.1 us -> none  [inject(): electric[2].at[first, second, third].add(jnp.where(inside, values, 0.0))]
    all_gather x1 -> x0, blocking collectives: 71.8 us -> none  [per_device(): samples = lax.all_gather(window, ('gx', 'gy', 'gz'), axis=0, tiled=True)]
    slice x66 -> x0, local copies, waits for them, and re-layouts: 45.9 us -> none  [the longest x45 26.8 us: shifted_above(): rest = lax.slice_in_dim(field, 1, field.shape[axis], axis=axis)]
    pallas_call x0 -> x1, Pallas kernels: none -> 43.1 us  [per_device(): pl.pallas_call(functools.partial(kernel, sizes), out_shape=(jax.ShapeDtyp...]
    psum x1 -> x0, blocking collectives: 42.1 us -> none  [per_device(): total = lax.psum(jnp.sum(gradient * gradient), ('gx', 'gy', 'gz'))]
    add x7 -> x0, other arithmetic: 22.9 us -> none  [the longest x6 19.9 us: local_step(): keep * electric_x]
    concatenate x4 -> x0, other arithmetic: 13 us -> none  [the longest x2 12 us: padded(): jnp.concatenate([lax.ppermute(tail, axis, [(i, (i + 1) % count) for i in...]
    sub x8 -> x0, other arithmetic: 9.74 us -> none  [the longest x5 6.79 us: local_step(): magnetic_z - halved * (shifted_above(electric_y, 0) - electric_y - (shift...]
  transfers between devices with their start and end apart: 6 -> 0, of which waited for: 3 -> 0; matrix products, arithmetic and copies ran while one was open for 3% -> 0% of each run, Pallas kernels for 0% -> 0%
where the time goes in v1:
time: 48.6 us; the launch traced here: 48.4 us
  Pallas kernels  43.1 us (89%)
  between operations  3.74 us (8%)
  local copies, waits for them, and re-layouts  1.57 us (3%)
    pallas_call x1, Pallas kernels, per_device(): pl.pallas_call(functools.partial(kernel, sizes), out_shape=(jax.ShapeDtyp...  43.1 us
    unnamed x1, local copies, waits for them, and re-layouts  1.57 us

profile of v1, /device:TPU:0, one launch (start us, length us, event | category | flops | bytes accessed | tf_op | source)
XLA Modules:
  0.0 48.4 jit_solution(322363363316694929)
XLA Ops:
  1.9 43.1 %shard_map.122 = (f32[8,32,128]{2,1,0:T(8,128)}, f32[1,1]{1,0:T(1,128)}) custom-call(f32[64]{0:T(128)} %wav_ref.1, s32[1]{0:T(128)S(6)} %copy.15.src_ref, s32[1]{0:T(128)S(6)} %copy.16.start_ref, s32[1,256]{1,0:T(1,128)} %bitcast.2, f32[8,32,128]{2,1,0:T(8,128)} %perm_hbm.1, f32[8,32,128]{2,1,0:T(8,128)} %loss_hbm.1, f32[3,8,32,128]{3,2,1,0:T(8,128)} %fe_hbm.1, ...), custom_call_target="tpu_custom_call" | custom-call | tf_op jit(solution)/shard_map/pallas_call | solution.py:408
  45.0 1.6 %copy.17 = f32[8,32,128]{2,1,0:T(8,128)} copy(f32[8,32,128]{2,1,0:T(8,128)} %get-tuple-element.8) | data formatting | bytes 262144

commit v2 on v1

--- a/solution.py
+++ b/solution.py
@@ -15,17 +15,17 @@
 
 def kernel(
     sizes,
-    wav_ref,
-    src_ref,
-    start_ref,
-    cells_ref,
+    wav_hbm,
+    src_hbm,
+    start_hbm,
+    cells_hbm,
     perm_hbm,
     loss_hbm,
     fe_hbm,
     fm_hbm,
     ae_hbm,
     am_hbm,
-    res_ref,
+    res_hbm,
     out_ref,
     rms_ref,
     E,
@@ -44,19 +44,20 @@
     zsend,
     zrecv,
     part,
-    suma,
-    sumb,
+    sums,
+    wav_ref,
+    src_ref,
+    start_ref,
+    cells_ref,
+    res_ref,
+    mine,
     load_sem,
     face_send,
     face_recv,
-    ga_send,
-    ga_recv,
-    gb_send,
-    gb_recv,
-    ra_send,
-    ra_recv,
-    rb_send,
-    rb_recv,
+    g_send,
+    g_recv,
+    r_send,
+    r_recv,
 ):
     gx, gy, gz = sizes
     nx, ny, nz = perm.shape
@@ -73,17 +74,26 @@
         pltpu.make_async_copy(loss_hbm, loss, load_sem.at[4]),
         pltpu.make_async_copy(perm_hbm, perm, load_sem.at[5]),
     ]
+    small = [
+        pltpu.make_async_copy(start_hbm, start_ref, load_sem.at[6]),
+        pltpu.make_async_copy(res_hbm, res_ref, load_sem.at[7]),
+        pltpu.make_async_copy(src_hbm, src_ref, load_sem.at[8]),
+        pltpu.make_async_copy(wav_hbm, wav_ref, load_sem.at[9]),
+        pltpu.make_async_copy(cells_hbm, cells_ref, load_sem.at[10]),
+    ]
+    loads = loads + small
+    for load in small:
+        load.start()
+    loads, small = loads[:6], loads[6:]
     for load in loads:
         load.start()
 
-    plane_peers = []
-    for d in range(1, nplane):
-        q = lax.rem(plane + d, nplane)
-        plane_peers.append((q, (ix, q // gz, lax.rem(q, gz))))
-    line_peers = []
-    for d in range(1, gx):
-        q = lax.rem(ix + d, gx)
-        line_peers.append((q, (q, iy, iz)))
+    total_devices = gx * nplane
+    me = ix * nplane + plane
+    peers = []
+    for d in range(1, total_devices):
+        q = lax.rem(me + d, total_devices)
+        peers.append((q, (q // nplane, lax.rem(q // gz, gy), lax.rem(q, gz))))
 
     zero_plane = jnp.zeros((ny, nz), F32)
     for s in range(2):
@@ -94,9 +104,24 @@
     zrecv[...] = jnp.zeros(zrecv.shape, F32)
 
     barrier = pltpu.get_barrier_semaphore()
-    for _, dev in plane_peers + line_peers:
+    for _, dev in peers:
         pl.semaphore_signal(barrier, inc=1, device_id=dev, device_id_type=MESH)
-    pl.semaphore_wait(barrier, len(plane_peers) + len(line_peers))
+
+    per, trace = res_hbm.shape
+    small[0].wait()
+    small[1].wait()
+    begin = start_ref[0]
+    time_at = lax.broadcasted_iota(jnp.int32, (trace, nz), 0)
+    slot = lax.div(lax.broadcasted_iota(jnp.int32, (trace, nz), 1), per)
+    pick = jnp.where(time_at == begin + STEPS - 1 - slot, 1.0, 0.0)
+    wide = jnp.dot(res_ref[...], pick, precision=lax.Precision.HIGHEST, preferred_element_type=F32)
+    own = lax.rem(lax.broadcasted_iota(jnp.int32, (per, nz), 1), per)
+    own = own == lax.broadcasted_iota(jnp.int32, (per, nz), 0)
+    mine[0] = jnp.sum(jnp.where(own, wide, 0.0), axis=0, keepdims=True)
+    R[pl.ds(me, 1)] = mine[...]
+    for load in small[2:]:
+        load.wait()
+    pl.semaphore_wait(barrier, len(peers))
 
     def remote(src, dst, ssem, rsem, dev):
         return pltpu.make_async_remote_copy(
@@ -104,31 +129,19 @@
             device_id=dev, device_id_type=MESH,
         )
 
-    per = res_ref.shape[0]
-
-    def rows_of(x, q, count):
-        return pl.ds(pl.multiple_of((x * nplane + q) * per, 8), count)
-
-    R[rows_of(ix, plane, per), :] = res_ref[...]
-    gather_a = []
-    for d, (q, dev) in enumerate(plane_peers):
-        send = remote(res_ref, R.at[rows_of(ix, plane, per), :], ga_send.at[d], ga_recv.at[plane], dev)
-        recv = remote(res_ref, R.at[rows_of(ix, q, per), :], ga_send.at[d], ga_recv.at[q], dev)
-        send.start()
-        gather_a.append((send, recv))
-
-    def gather_mid():
-        for send, recv in gather_a:
+    def exchange(src, slots, send_sems, recv_sems):
+        copies = []
+        for d, (q, dev) in enumerate(peers):
+            send = remote(src, slots.at[me], send_sems.at[d], recv_sems.at[me], dev)
+            recv = remote(src, slots.at[q], send_sems.at[d], recv_sems.at[q], dev)
+            send.start()
+            copies.append((send, recv))
+        return copies
+
+    def settle(copies):
+        for send, recv in copies:
             recv.wait_recv()
-        for d, (q, dev) in enumerate(line_peers):
-            mine = R.at[rows_of(ix, 0, per * nplane), :]
-            remote(mine, mine, gb_send.at[d], gb_recv.at[ix], dev).start()
-
-    def gather_end():
-        for d, (q, dev) in enumerate(line_peers):
-            theirs = R.at[rows_of(q, 0, per * nplane), :]
-            remote(theirs, theirs, gb_send.at[d], gb_recv.at[q], dev).wait()
-        for send, recv in gather_a:
+        for send, recv in copies:
             send.wait_send()
 
     def faces(s, kind):
@@ -234,7 +247,6 @@
         start(going[2])
 
     src = src_ref[0]
-    begin = start_ref[0]
     total_z, total_y = nz * gz, ny * gy
     src_i = lax.div(src, total_y * total_z) - ix * nx
     src_j = lax.rem(lax.div(src, total_z), total_y) - iy * ny
@@ -303,14 +315,17 @@
         rows = lax.broadcasted_iota(jnp.int32, (nx * ny, count), 0)
         spots = jnp.where(rows == where, 1.0, 0.0).astype(jnp.bfloat16)
         depth = lax.broadcasted_iota(jnp.int32, (nz, count), 0) == k
-        trace = R.shape[1]
-        pick_lane = lax.broadcasted_iota(jnp.int32, (8, trace), 1)
-        pick_row = lax.broadcasted_iota(jnp.int32, (8, trace), 0)
-        pick = jnp.where(pick_lane == begin + STEPS - 1 - pick_row, 1.0, 0.0)
         nt = (((1,), (1,)), ((), ()))
-        samples = lax.dot_general(pick, R[...], nt, precision=lax.Precision.HIGHEST, preferred_element_type=F32)
+        spread_lane = lax.broadcasted_iota(jnp.int32, (nz, count), 0)
+        spread_rec = lax.rem(lax.broadcasted_iota(jnp.int32, (nz, count), 1), per)
+        holder = lax.div(lax.broadcasted_iota(jnp.int32, (total_devices, count), 1), per)
+        holder = holder == lax.broadcasted_iota(jnp.int32, (total_devices, count), 0)
+        packed = R[:, 0, :]
         for m in range(STEPS):
-            rest = jnp.where(depth, samples[m : m + 1, :], 0.0)
+            spread = jnp.where(spread_lane == m * per + spread_rec, 1.0, 0.0)
+            found = jnp.dot(packed, spread, precision=lax.Precision.HIGHEST, preferred_element_type=F32)
+            samples = jnp.sum(jnp.where(holder, found, 0.0), axis=0, keepdims=True)
+            rest = jnp.where(depth, samples, 0.0)
             total = jnp.zeros((nx * ny, nz), F32)
             for _ in range(3):
                 head = rest.astype(jnp.bfloat16)
@@ -322,6 +337,7 @@
     send_first(0)
     loads[1].wait()
     send_first(1)
+    gather = exchange(mine.at[0], R, g_send, g_recv)
     loads[4].wait()
     loads[5].wait()
     for p in range(nx):
@@ -332,10 +348,9 @@
     loads[3].wait()
 
     update_h(0)
-    gather_mid()
     update_h(1)
     update_e(0, 0)
-    gather_end()
+    settle(gather)
     injection()
     update_e(1, 0)
 
@@ -357,30 +372,10 @@
         g = -total / perm[p]
         grad[p] = g
         squares = squares + g * g
-    tile = squares[0:8, :]
-    for r in range(1, ny // 8):
-        tile = tile + squares[8 * r : 8 * r + 8, :]
-    part[0] = tile
-
-    def reduce(src, slots, me, peers, send_sems, recv_sems, count):
-        slots[pl.ds(me, 1)] = src[...][None]
-        copies = []
-        for d, (q, dev) in enumerate(peers):
-            send = remote(src, slots.at[me], send_sems.at[d], recv_sems.at[me], dev)
-            recv = remote(src, slots.at[q], send_sems.at[d], recv_sems.at[q], dev)
-            send.start()
-            copies.append((send, recv))
-        for send, recv in copies:
-            recv.wait_recv()
-        out = slots[0]
-        for q in range(1, count):
-            out = out + slots[q]
-        for send, recv in copies:
-            send.wait_send()
-        return out
-
-    part[1] = reduce(part.at[0], suma, plane, plane_peers, ra_send, ra_recv, nplane)
-    tile = reduce(part.at[1], sumb, ix, line_peers, rb_send, rb_recv, gx)
+    part[0] = jnp.sum(squares, axis=0, keepdims=True)
+    sums[pl.ds(me, 1)] = part[...]
+    settle(exchange(part.at[0], sums, r_send, r_recv))
+    tile = sums[:, 0, :]
     total = jnp.sum(jnp.sum(tile, axis=0, keepdims=True), axis=1, keepdims=True)
     rms = jnp.sqrt(total / (nx * ny * nz * gx * gy * gz) + 1e-06)
     rms_ref[...] = rms
@@ -396,22 +391,20 @@
     sizes = tuple(lax.axis_size(a) for a in ("gx", "gy", "gz"))
     gx, gy, gz = sizes
     nx, ny, nz = permittivity.shape
-    nplane = gy * gz
+    devices = gx * gy * gz
     count = receiver_cells.shape[0]
-    trace = residuals.shape[1]
-    smem = pl.BlockSpec(memory_space=pltpu.SMEM)
     vmem = pl.BlockSpec(memory_space=pltpu.VMEM)
-    hbm = pl.BlockSpec(memory_space=pl.ANY)
+    hbm = pl.BlockSpec(memory_space=pltpu.HBM)
     dma = pltpu.SemaphoreType.DMA
     block = (nx, ny, nz)
     padded = (2, 3, nx + 1, ny + 8, nz)
     direction, rms = pl.pallas_call(
         functools.partial(kernel, sizes),
         out_shape=(
-            jax.ShapeDtypeStruct(block, F32),
+            pltpu.VMEM(block, F32),
             jax.ShapeDtypeStruct((1, 1), F32),
         ),
-        in_specs=[smem, smem, smem, vmem, hbm, hbm, hbm, hbm, hbm, hbm, vmem],
+        in_specs=[hbm] * 11,
         out_specs=(vmem, vmem),
         scratch_shapes=[
             pltpu.VMEM(padded, F32),
@@ -423,26 +416,27 @@
             pltpu.VMEM((STEPS, 3) + block, F32),
             pltpu.VMEM((STEPS, 3) + block, F32),
             pltpu.VMEM((STEPS, nx * ny, nz), F32),
-            pltpu.VMEM((count, trace), F32),
+            pltpu.VMEM((devices, 1, nz), F32),
             pltpu.VMEM(block, F32),
             pltpu.VMEM((2, 2, 2, nx, nz), F32),
             pltpu.VMEM((2, 2, 2, nx, nz), F32),
             pltpu.VMEM((2, 2, ny, nz), F32),
             pltpu.VMEM((2, 2, ny, nz), F32),
-            pltpu.VMEM((2, 8, nz), F32),
-            pltpu.VMEM((nplane, 8, nz), F32),
-            pltpu.VMEM((gx, 8, nz), F32),
-            dma((6,)),
+            pltpu.VMEM((1, 1, nz), F32),
+            pltpu.VMEM((devices, 1, nz), F32),
+            pltpu.SMEM(wavelet.shape, F32),
+            pltpu.SMEM((1,), jnp.int32),
+            pltpu.SMEM((1,), jnp.int32),
+            pltpu.VMEM((1, count), jnp.int32),
+            pltpu.VMEM(residuals.shape, F32),
+            pltpu.VMEM((1, 1, nz), F32),
+            dma((11,)),
             dma((2, 2, 3)),
             dma((2, 2, 3)),
-            dma((nplane,)),
-            dma((nplane,)),
-            dma((gx,)),
-            dma((gx,)),
-            dma((nplane,)),
-            dma((nplane,)),
-            dma((gx,)),
-            dma((gx,)),
+            dma((devices,)),
+            dma((devices,)),
+            dma((devices,)),
+            dma((devices,)),
         ],
         compiler_params=pltpu.CompilerParams(
             collective_id=0, has_side_effects=True, vmem_limit_bytes=60 * 1024 * 1024

time: 48.6 us -> 44.5 us (0.916)
  Pallas kernels: 43.1 us -> 40.1 us
  local copies, waits for them, and re-layouts: 1.57 us -> 0.66 us
    pallas_call x1, Pallas kernels: 43.1 us -> 40.1 us  [per_device(): pl.pallas_call(functools.partial(kernel, sizes), out_shape=(pltpu.VMEM(bl...]
    unnamed x1, local copies, waits for them, and re-layouts: 1.57 us -> 0.66 us
where the time goes in v2:
time: 44.5 us; the launch traced here: 44.4 us
  Pallas kernels  40.1 us (90%)
  between operations  3.62 us (8%)
  local copies, waits for them, and re-layouts  0.66 us (1%)
    pallas_call x1, Pallas kernels, per_device(): pl.pallas_call(functools.partial(kernel, sizes), out_shape=(pltpu.VMEM(bl...  40.1 us

profile of v2, /device:TPU:0, one launch (start us, length us, event | category | flops | bytes accessed | tf_op | source)
XLA Modules:
  0.0 44.4 jit_solution(3022605681039413249)
XLA Ops:
  1.9 40.1 %shard_map.122 = (f32[8,32,128]{2,1,0:T(8,128)S(1)}, f32[1,1]{1,0:T(1,128)}) custom-call(f32[64]{0:T(128)} %wav_hbm.1, s32[1]{0:T(128)S(6)} %copy.16.src_hbm, s32[1]{0:T(128)S(6)} %copy.17.start_hbm, s32[1,256]{1,0:T(1,128)} %bitcast.2, f32[8,32,128]{2,1,0:T(8,128)} %perm_hbm.1, f32[8,32,128]{2,1,0:T(8,128)} %loss_hbm.1, f32[3,8,32,128]{3,2,1,0:T(8,128)} %fe_hbm.1, ...), custom_call_target="tpu_custom_call" | custom-call | tf_op jit(solution)/shard_map/pallas_call | solution.py:401
  42.0 0.7 %copy.15 = f32[8,32,128]{2,1,0:T(8,128)} copy(f32[8,32,128]{2,1,0:T(8,128)S(1)} %get-tuple-element.6) | data formatting | bytes 262144

commit v3 on v2

--- a/solution.py
+++ b/solution.py
@@ -208,11 +208,16 @@
         acc = jnp.zeros((ny, nz), F32)
         face = faces(s, 0)
         start(face[0])
-        for p in range(nx):
-            ysend[0, s, 0, p : p + 1, :] = E[s, 0, p, 0:1, :]
-            ysend[0, s, 1, p : p + 1, :] = E[s, 2, p, 0:1, :]
-            acc = pack_column(acc, E[s, 0, p, 0:ny, :], 0, p)
-            acc = pack_column(acc, E[s, 1, p, 0:ny, :], 0, nx + p)
+        def planes(t, acc):
+            for u in range(2):
+                p = 2 * t + u
+                ysend[0, s, 0, p] = E[s, 0, p, 0:1, :]
+                ysend[0, s, 1, p] = E[s, 2, p, 0:1, :]
+                acc = pack_column(acc, E[s, 0, p, 0:ny, :], 0, p)
+                acc = pack_column(acc, E[s, 1, p, 0:ny, :], 0, nx + p)
+            return acc
+
+        acc = lax.fori_loop(0, nx // 2, planes, acc)
         zsend[0, s] = acc
         start(face[1])
         start(face[2])
@@ -223,25 +228,33 @@
         for face in came:
             arrive(face)
         for p in range(nx):
-            E[s, 0, p, ny : ny + 1, :] = yrecv[0, s, 0, p : p + 1, :]
-            E[s, 2, p, ny : ny + 1, :] = yrecv[0, s, 1, p : p + 1, :]
+            E[s, 0, p, ny : ny + 1, :] = yrecv[0, s, 0, p]
+            E[s, 2, p, ny : ny + 1, :] = yrecv[0, s, 1, p]
         halo = zrecv[0, s]
         acc = jnp.zeros((ny, nz), F32)
         inner = slice(pad, pad + ny)
-        for p in reversed(range(nx)):
-            ex, ey, ez = E[s, 0, p, 0:ny, :], E[s, 1, p, 0:ny, :], E[s, 2, p, 0:ny, :]
-            hx = H[s, 0, p + 1, inner, :] - HALF * (E[s, 2, p, 1 : ny + 1, :] - ez - (up_z(ey, halo, nx + p) - ey))
-            hy = H[s, 1, p + 1, inner, :] - HALF * (up_z(ex, halo, p) - ex - (E[s, 2, p + 1, 0:ny, :] - ez))
-            hz = H[s, 2, p + 1, inner, :] - HALF * (E[s, 1, p + 1, 0:ny, :] - ey - (E[s, 0, p, 1 : ny + 1, :] - ex))
-            H[s, 0, p + 1, inner, :] = hx
-            H[s, 1, p + 1, inner, :] = hy
-            H[s, 2, p + 1, inner, :] = hz
-            if p == nx - 1:
+        def planes(t, acc):
+            for u in range(2):
+                p = nx - 1 - (2 * t + u)
+                ex, ey, ez = E[s, 0, p, 0:ny, :], E[s, 1, p, 0:ny, :], E[s, 2, p, 0:ny, :]
+                hx = H[s, 0, p + 1, inner, :] - HALF * (E[s, 2, p, 1 : ny + 1, :] - ez - (up_z(ey, halo, nx + p) - ey))
+                hy = H[s, 1, p + 1, inner, :] - HALF * (up_z(ex, halo, p) - ex - (E[s, 2, p + 1, 0:ny, :] - ez))
+                hz = H[s, 2, p + 1, inner, :] - HALF * (E[s, 1, p + 1, 0:ny, :] - ey - (E[s, 0, p, 1 : ny + 1, :] - ex))
+                H[s, 0, p + 1, inner, :] = hx
+                H[s, 1, p + 1, inner, :] = hy
+                H[s, 2, p + 1, inner, :] = hz
+                ysend[1, s, 0, p] = hx[ny - 1 : ny, :]
+                ysend[1, s, 1, p] = hz[ny - 1 : ny, :]
+                acc = pack_column(acc, hx, nz - 1, p)
+                acc = pack_column(acc, hy, nz - 1, nx + p)
+
+            @pl.when(t == 0)
+            def _():
                 start(going[0])
-            ysend[1, s, 0, p : p + 1, :] = hx[ny - 1 : ny, :]
-            ysend[1, s, 1, p : p + 1, :] = hz[ny - 1 : ny, :]
-            acc = pack_column(acc, hx, nz - 1, p)
-            acc = pack_column(acc, hy, nz - 1, nx + p)
+
+            return acc
+
+        acc = lax.fori_loop(0, nx // 2, planes, acc)
         zsend[1, s] = acc
         start(going[1])
         start(going[2])
@@ -261,40 +274,48 @@
         for face in going:
             finish(face)
         for p in range(nx):
-            H[s, 0, p + 1, pad - 1 : pad, :] = yrecv[1, s, 0, p : p + 1, :]
-            H[s, 2, p + 1, pad - 1 : pad, :] = yrecv[1, s, 1, p : p + 1, :]
+            H[s, 0, p + 1, pad - 1 : pad, :] = yrecv[1, s, 0, p]
+            H[s, 2, p + 1, pad - 1 : pad, :] = yrecv[1, s, 1, p]
         more = k < STEPS - 1
         halo = zrecv[1, s]
         acc = jnp.zeros((ny, nz), F32)
         inner = slice(pad, pad + ny)
         below = slice(pad - 1, pad + ny - 1)
         pulse = wav_ref[begin + k]
-        for p in range(nx):
-            hx, hy, hz = H[s, 0, p + 1, inner, :], H[s, 1, p + 1, inner, :], H[s, 2, p + 1, inner, :]
-            kp, cl = keep[p], curl[p]
-            ox, oy, oz = E[s, 0, p, 0:ny, :], E[s, 1, p, 0:ny, :], E[s, 2, p, 0:ny, :]
-            ex = kp * ox + cl * (hz - H[s, 2, p + 1, below, :] - (hy - down_z(hy, halo, nx + p)))
-            ey = kp * oy + cl * (hx - down_z(hx, halo, p) - (hz - H[s, 2, p, inner, :]))
-            ez = kp * oz + cl * (hy - H[s, 1, p, inner, :] - (hx - H[s, 0, p + 1, below, :]))
-            if s == 0:
-                ez = ez + jnp.where(src_mask, jnp.where(src_i == p, pulse, 0.0), 0.0)
-                D[k, 0, p] = ex - ox
-                D[k, 1, p] = ey - oy
-                D[k, 2, p] = ez - oz
-            else:
-                ez = ez + inj[k, p * ny : (p + 1) * ny, :]
-                A[k, 0, p] = ex
-                A[k, 1, p] = ey
-                A[k, 2, p] = ez
-            E[s, 0, p, 0:ny, :] = ex
-            E[s, 1, p, 0:ny, :] = ey
-            E[s, 2, p, 0:ny, :] = ez
-            if p == 0:
+        def planes(t, acc):
+            for u in range(2):
+                p = 2 * t + u
+                hx, hy, hz = H[s, 0, p + 1, inner, :], H[s, 1, p + 1, inner, :], H[s, 2, p + 1, inner, :]
+                kp, cl = keep[p], curl[p]
+                ox, oy, oz = E[s, 0, p, 0:ny, :], E[s, 1, p, 0:ny, :], E[s, 2, p, 0:ny, :]
+                ex = kp * ox + cl * (hz - H[s, 2, p + 1, below, :] - (hy - down_z(hy, halo, nx + p)))
+                ey = kp * oy + cl * (hx - down_z(hx, halo, p) - (hz - H[s, 2, p, inner, :]))
+                ez = kp * oz + cl * (hy - H[s, 1, p, inner, :] - (hx - H[s, 0, p + 1, below, :]))
+                if s == 0:
+                    ez = ez + jnp.where(src_mask, jnp.where(src_i == p, pulse, 0.0), 0.0)
+                    D[k, 0, p] = ex - ox
+                    D[k, 1, p] = ey - oy
+                    D[k, 2, p] = ez - oz
+                else:
+                    ez = ez + inj[k, pl.ds(pl.multiple_of(p * ny, 8), ny), :]
+                    A[k, 0, p] = ex
+                    A[k, 1, p] = ey
+                    A[k, 2, p] = ez
+                E[s, 0, p, 0:ny, :] = ex
+                E[s, 1, p, 0:ny, :] = ey
+                E[s, 2, p, 0:ny, :] = ez
+                ysend[0, s, 0, p] = ex[0:1, :]
+                ysend[0, s, 1, p] = ez[0:1, :]
+                acc = pack_column(acc, ex, 0, p)
+                acc = pack_column(acc, ey, 0, nx + p)
+
+            @pl.when(t == 0)
+            def _():
                 start(going[0], more)
-            ysend[0, s, 0, p : p + 1, :] = ex[0:1, :]
-            ysend[0, s, 1, p : p + 1, :] = ez[0:1, :]
-            acc = pack_column(acc, ex, 0, p)
-            acc = pack_column(acc, ey, 0, nx + p)
+
+            return acc
+
+        acc = lax.fori_loop(0, nx // 2, planes, acc)
         zsend[0, s] = acc
         start(going[1], more)
         start(going[2], more)
@@ -363,15 +384,16 @@
 
     lax.fori_loop(1, STEPS, body, 0)
 
-    squares = jnp.zeros((ny, nz), F32)
-    for p in range(nx):
+    def correlate(p, squares):
         total = jnp.zeros((ny, nz), F32)
         for m in range(STEPS):
             n = STEPS - 1 - m
             total = total + (D[n, 0, p] * A[m, 0, p] + D[n, 1, p] * A[m, 1, p] + D[n, 2, p] * A[m, 2, p])
         g = -total / perm[p]
         grad[p] = g
-        squares = squares + g * g
+        return squares + g * g
+
+    squares = lax.fori_loop(0, nx, correlate, jnp.zeros((ny, nz), F32))
     part[0] = jnp.sum(squares, axis=0, keepdims=True)
     sums[pl.ds(me, 1)] = part[...]
     settle(exchange(part.at[0], sums, r_send, r_recv))
@@ -418,8 +440,8 @@
             pltpu.VMEM((STEPS, nx * ny, nz), F32),
             pltpu.VMEM((devices, 1, nz), F32),
             pltpu.VMEM(block, F32),
-            pltpu.VMEM((2, 2, 2, nx, nz), F32),
-            pltpu.VMEM((2, 2, 2, nx, nz), F32),
+            pltpu.VMEM((2, 2, 2, nx, 1, nz), F32),
+            pltpu.VMEM((2, 2, 2, nx, 1, nz), F32),
             pltpu.VMEM((2, 2, ny, nz), F32),
             pltpu.VMEM((2, 2, ny, nz), F32),
             pltpu.VMEM((1, 1, nz), F32),

time: 44.5 us -> 46.8 us (1.052)
  Pallas kernels: 40.1 us -> 42.3 us
    pallas_call x1, Pallas kernels: 40.1 us -> 42.3 us  [per_device(): pl.pallas_call(functools.partial(kernel, sizes), out_shape=(pltpu.VMEM(bl...]
where the time goes in v3:
time: 46.8 us; the launch traced here: 46.6 us
  Pallas kernels  42.3 us (90%)
  between operations  3.62 us (8%)
  local copies, waits for them, and re-layouts  0.66 us (1%)
    pallas_call x1, Pallas kernels, per_device(): pl.pallas_call(functools.partial(kernel, sizes), out_shape=(pltpu.VMEM(bl...  42.3 us

profile of v3, /device:TPU:0, one launch (start us, length us, event | category | flops | bytes accessed | tf_op | source)
XLA Modules:
  0.0 46.6 jit_solution(17957252752320106352)
XLA Ops:
  1.9 42.3 %shard_map.122 = (f32[8,32,128]{2,1,0:T(8,128)S(1)}, f32[1,1]{1,0:T(1,128)}) custom-call(f32[64]{0:T(128)} %wav_hbm.1, s32[1]{0:T(128)S(6)} %copy.16.src_hbm, s32[1]{0:T(128)S(6)} %copy.17.start_hbm, s32[1,256]{1,0:T(1,128)} %bitcast.2, f32[8,32,128]{2,1,0:T(8,128)} %perm_hbm.1, f32[8,32,128]{2,1,0:T(8,128)} %loss_hbm.1, f32[3,8,32,128]{3,2,1,0:T(8,128)} %fe_hbm.1, ...), custom_call_target="tpu_custom_call" | custom-call | tf_op jit(solution)/shard_map/pallas_call | solution.py:423
  44.2 0.7 %copy.15 = f32[8,32,128]{2,1,0:T(8,128)} copy(f32[8,32,128]{2,1,0:T(8,128)S(1)} %get-tuple-element.6) | data formatting | bytes 262144
